TPU v7x, 128 devices: a whole 4x4x4 slice. The times are simulated.
128 devices in a mesh: tp: 2 (over core), dp: 64 (over z, y, x).
Axes of the slice: x: 4, y: 4, z: 4, core: 2. Of those that a mesh axis runs over, the one named last changes fastest.
Arguments:
- x_tokens: bfloat16 [16384, 2048], P('dp')
- dh_out: bfloat16 [16384, 2048], P('dp')
- w_in: bfloat16 [2, 2048, 8192], P(None, None, 'tp')
- w_out: bfloat16 [2, 8192, 2048], P(None, 'tp')
- p_in: bfloat16 [2, 2048, 256], replicated
- q_out: bfloat16 [2, 2048, 256], replicated
- m_in: float32 [2, 256, 8192], P(None, None, ('tp', 'dp'))
- v_in: float32 [2, 256, 8192], P(None, None, ('tp', 'dp'))
- m_out: float32 [2, 8192, 256], P(None, ('tp', 'dp'))
- v_out: float32 [2, 8192, 256], P(None, ('tp', 'dp'))
Outputs:
- output 1: bfloat16 [2, 2048, 8192], P(None, None, 'tp')
- output 2: bfloat16 [2, 8192, 2048], P(None, 'tp')
- output 3: float32 [2, 256, 8192], P(None, None, ('tp', 'dp'))
- output 4: float32 [2, 256, 8192], P(None, None, ('tp', 'dp'))
- output 5: float32 [2, 8192, 256], P(None, ('tp', 'dp'))
- output 6: float32 [2, 8192, 256], P(None, ('tp', 'dp'))
All inputs are finite; a program needn't handle non-finite values.
Results may differ from a plain program's by a relative error of at most 0.0108964.
Values are sent between devices in bfloat16 or wider.
A program may use at most 1 GiB of HBM per device.

v0:
```python
import jax
import jax.numpy as jnp
from jax import lax
from jax.sharding import PartitionSpec as P, NamedSharding

BETA1 = 0.9
BETA2 = 0.999
EPSILON = 1e-8
STEP = 2
STEP_SIZE = 0.03 * 0.25
CORR_MOM = 1.0 - BETA1 ** STEP
CORR_VAR = 1.0 - BETA2 ** STEP


def contract(left_op, right_op, left_dim, right_dim):
    return lax.dot_general(left_op, right_op, (((left_dim,), (right_dim,)), ((), ())), preferred_element_type=jnp.float32)


def contract_exact(left_op, right_op, left_dim, right_dim):
    return lax.dot_general(left_op, right_op, (((left_dim,), (right_dim,)), ((), ())), precision=lax.Precision.HIGHEST, preferred_element_type=jnp.float32)


def adam_direction(grad_proj, moment, second):
    moment_new = BETA1 * moment + (1.0 - BETA1) * grad_proj
    second_new = BETA2 * second + (1.0 - BETA2) * grad_proj * grad_proj
    direction = (moment_new / CORR_MOM) / (jnp.sqrt(second_new / CORR_VAR) + EPSILON)
    return direction.astype(jnp.bfloat16), moment_new, second_new


def forward_backward(x_rows, g_rows, w_in, w_out):
    layers = w_in.shape[0]
    states = [x_rows]
    activations = []
    gelu_vjps = []
    for layer_idx in range(layers):
        pre_act = jnp.dot(states[-1], w_in[layer_idx], preferred_element_type=jnp.float32).astype(jnp.bfloat16)
        act_f32, gelu_vjp = jax.vjp(jax.nn.gelu, pre_act.astype(jnp.float32))
        act_bf16 = act_f32.astype(jnp.bfloat16)
        activations.append(act_bf16)
        gelu_vjps.append(gelu_vjp)
        if layer_idx < layers - 1:
            mlp_out = lax.psum(jnp.dot(act_bf16, w_out[layer_idx], preferred_element_type=jnp.float32), "tp")
            states.append((states[-1].astype(jnp.float32) + mlp_out).astype(jnp.bfloat16))
    grads_in = [None] * layers
    grads_out = [None] * layers
    cotangent = g_rows
    for layer_idx in reversed(range(layers)):
        grads_out[layer_idx] = contract(activations[layer_idx], cotangent, 0, 0)
        d_act = contract(cotangent, w_out[layer_idx], 1, 1)
        d_pre = gelu_vjps[layer_idx](d_act)[0].astype(jnp.bfloat16)
        grads_in[layer_idx] = contract(states[layer_idx], d_pre, 0, 0)
        if layer_idx > 0:
            back_sum = lax.psum(contract(d_pre, w_in[layer_idx], 1, 1), "tp")
            cotangent = (cotangent.astype(jnp.float32) + back_sum).astype(jnp.bfloat16)
    return grads_in, grads_out


def solution(mesh):
    weight_in_spec = P(None, None, "tp")
    weight_out_spec = P(None, "tp", None)
    moment_in_spec = P(None, None, ("tp", "dp"))
    moment_out_spec = P(None, ("tp", "dp"), None)

    def local_step(x_rows, g_rows, w_in, w_out, p_in, q_out, m_in, v_in, m_out, v_out):
        grads_in, grads_out = forward_backward(x_rows, g_rows, w_in, w_out)
        results = [[], [], [], [], [], []]
        for layer_idx in range(w_in.shape[0]):
            proj_in = contract_exact(p_in[layer_idx].astype(jnp.float32), grads_in[layer_idx], 0, 0)
            proj_out = contract_exact(grads_out[layer_idx], q_out[layer_idx].astype(jnp.float32), 1, 0)
            shard_in = lax.psum_scatter(proj_in, "dp", scatter_dimension=1, tiled=True)
            shard_out = lax.psum_scatter(proj_out, "dp", scatter_dimension=0, tiled=True)
            dir_in, mom_in, var_in = adam_direction(shard_in, m_in[layer_idx], v_in[layer_idx])
            dir_out, mom_out, var_out = adam_direction(shard_out, m_out[layer_idx], v_out[layer_idx])
            full_in = lax.all_gather(dir_in, "dp", axis=1, tiled=True)
            full_out = lax.all_gather(dir_out, "dp", axis=0, tiled=True)
            upd_in = jnp.dot(p_in[layer_idx], full_in, preferred_element_type=jnp.float32)
            upd_out = contract(full_out, q_out[layer_idx], 1, 1)
            results[0].append((w_in[layer_idx].astype(jnp.float32) - STEP_SIZE * upd_in).astype(jnp.bfloat16))
            results[1].append((w_out[layer_idx].astype(jnp.float32) - STEP_SIZE * upd_out).astype(jnp.bfloat16))
            results[2].append(mom_in)
            results[3].append(var_in)
            results[4].append(mom_out)
            results[5].append(var_out)
        return tuple(jnp.stack(collected) for collected in results)

    return jax.shard_map(local_step, mesh=mesh, in_specs=(P("dp", None), P("dp", None), weight_in_spec, weight_out_spec, P(), P(), moment_in_spec, moment_in_spec, moment_out_spec, moment_out_spec), out_specs=(weight_in_spec, weight_out_spec, moment_in_spec, moment_in_spec, moment_out_spec, moment_out_spec), check_vma=False)
```

profile of v0, /device:TPU:0, one launch (start us, length us, event | category | flops | bytes accessed | tf_op | source)
XLA Modules:
  0.0 1888.8 jit_solution(14632726126280256975)
XLA Ops:
  7.2 0.0 all-reduce.3.cloned.1.call-start
  7.2 10.6 fusion.23
  17.8 12.1 fusion.14
  29.9 0.0 all-reduce.3.cloned.1.call-update
  29.9 0.0 copy-start
  29.9 0.5 all-reduce.5.cloned.1.call-start
  30.5 28.2 %all-reduce.3.cloned.1.call-done = f32[256,2048]{1,0:T(8,128)} async-done(((f32[256,2048]{1,0:T(8,128)}), f32[256,2048]{1,0:T(8,128)}) %all-reduce.3.cloned.1.call-update) | async-done | bytes 2097168 | tf_op jit(solution)/shard_map/psum | solution.py:42
  58.7 11.2 fusion.26
  69.9 0.0 copy-start.1
  69.9 1.3 copy-done.1
  71.2 0.0 copy-done
  71.2 11.2 fusion.31
  82.5 12.2 fusion.6
  94.7 0.0 all-reduce.5.cloned.1.call-update
  94.7 0.0 reduce-scatter.7.cloned.1.call-start
  94.8 18.8 fusion.106
  113.6 34.5 %convolution_bitcast_fusion = f32[256,4096]{0,1:T(8,128)} fusion(f32[2048,4096]{1,0:T(8,128)} %fusion.106, bf16[2,2048,256]{2,1,0:T(8,128)(2,1)} %param.14), kind=kOutput, calls=%fused_computation.39 | convolution fusion | flops 25769803776 | bytes 38797312 | tf_op jit(solution)/shard_map/dot_general | solution.py:20
  148.1 0.0 reduce-scatter.7.cloned.1.call-update
  148.1 0.0 reduce-scatter.5.cloned.1.call-start
  148.1 0.0 all-reduce.5.cloned.1.call-done
  148.2 21.9 %fusion.52 = f32[4096,2048]{1,0:T(8,128)} fusion(bf16[256,2048]{1,0:T(8,128)(2,1)} %param.10, bf16[256,4096]{1,0:T(8,128)(2,1)S(1)} %fusion.23, bf16[2,4096,2048]{2,1,0:T(8,128)(2,1)} %param.13, f32[256,2048]{1,0:T(8,128)} %all-reduce.5.cloned.1.call-done, bf16[256,2048]{1,0:T(8,128)(2,1)S(1)} %copy-done), kind=kOutput, calls=%fused_computation.61 | convolution fusion | flops 8613527552 | bytes 56623104 | tf_op jit(solution)/shard_map/dot_general | solution.py:16
  170.1 19.8 %convolution_bitcast_fusion.1 = f32[256,4096]{0,1:T(8,128)} fusion(f32[4096,2048]{1,0:T(8,128)} %fusion.52, bf16[2,2048,256]{2,1,0:T(8,128)(2,1)} %param.14), kind=kOutput, calls=%fused_computation.40 | convolution fusion | flops 25769803776 | bytes 38797312 | tf_op jit(solution)/shard_map/dot_general | solution.py:20
  189.9 0.0 reduce-scatter.5.cloned.1.call-update
  189.9 0.0 reduce-scatter.11.cloned.1.call-start
  190.0 16.4 fusion.54
  206.3 19.8 %fusion.67 = f32[4096,256]{1,0:T(8,128)} fusion(f32[4096,2048]{1,0:T(8,128)} %fusion.54, bf16[2,2048,256]{2,1,0:T(8,128)(2,1)} %param.15), kind=kOutput, calls=%fused_computation.76 | convolution fusion | flops 25769803776 | bytes 38797312 | tf_op jit(solution)/shard_map/dot_general | solution.py:20
  226.1 0.0 reduce-scatter.11.cloned.1.call-update
  226.2 0.0 reduce-scatter.9.cloned.1.call-start
  226.2 16.2 fusion.107
  242.4 19.8 %fusion.70 = f32[4096,256]{1,0:T(8,128)} fusion(f32[4096,2048]{1,0:T(8,128)} %fusion.107, bf16[2,2048,256]{2,1,0:T(8,128)(2,1)} %param.15), kind=kOutput, calls=%fused_computation.79 | convolution fusion | flops 25769803776 | bytes 38797312 | tf_op jit(solution)/shard_map/dot_general | solution.py:20
  262.2 0.0 copy-start.7
  262.2 0.0 reduce-scatter.9.cloned.1.call-update
  262.3 0.0 all-gather.5.cloned.1.call-start
  262.3 248.6 %reduce-scatter.7.cloned.1.call-done = f32[256,64]{0,1:T(8,128)} async-done(((f32[256,4096]{0,1:T(8,128)}), f32[256,64]{0,1:T(8,128)}) %reduce-scatter.7.cloned.1.call-update) | async-done | bytes 65552 | tf_op jit(solution)/shard_map/reduce_scatter | solution.py:70
  510.9 358.7 %reduce-scatter.5.cloned.1.call-done = f32[256,64]{0,1:T(8,128)} async-done(((f32[256,4096]{0,1:T(8,128)}), f32[256,64]{0,1:T(8,128)}) %reduce-scatter.5.cloned.1.call-update) | async-done | bytes 65552 | tf_op jit(solution)/shard_map/reduce_scatter | solution.py:70
  869.6 0.0 copy-done.4
  869.6 0.0 copy-done.5
  869.6 1.6 divide_convert_fusion.3
  871.2 0.0 all-gather.5.cloned.1.call-update
  871.2 0.0 all-gather.7.cloned.1.call-start
  871.2 0.7 all-gather.7.cloned.1.call-update
  872.0 0.0 all-gather.11.cloned.1.call-start
  872.0 355.7 %reduce-scatter.11.cloned.1.call-done = f32[64,256]{1,0:T(8,128)} async-done(((f32[4096,256]{1,0:T(8,128)}), f32[64,256]{1,0:T(8,128)}) %reduce-scatter.11.cloned.1.call-update) | async-done | bytes 65552 | tf_op jit(solution)/shard_map/reduce_scatter | solution.py:71
  1227.7 358.2 %reduce-scatter.9.cloned.1.call-done = f32[64,256]{1,0:T(8,128)} async-done(((f32[4096,256]{1,0:T(8,128)}), f32[64,256]{1,0:T(8,128)}) %reduce-scatter.9.cloned.1.call-update) | async-done | bytes 65552 | tf_op jit(solution)/shard_map/reduce_scatter | solution.py:71
  1585.9 0.0 copy-done.6
  1585.9 1.6 divide_convert_fusion.1
  1587.5 0.0 all-gather.11.cloned.1.call-update
  1587.5 0.0 all-gather.9.cloned.1.call-start
  1587.6 23.4 %fusion.113 = (bf16[1,2048,4096]{2,1,0:T(8,128)(2,1)}, bf16[1,2048,4096]{2,1,0:T(8,128)(2,1)}) fusion(bf16[2,2048,4096]{2,1,0:T(8,128)(2,1)} %param.12), kind=kLoop, calls=%fused_computation.136 | loop fusion | bytes 67108864 | tf_op jit(solution)/shard_map/slice | solution.py:78
  1611.0 22.6 %copy.19 = bf16[1,2048,4096]{1,2,0:T(8,128)(2,1)} copy(bf16[1,2048,4096]{2,1,0:T(8,128)(2,1)} %get-tuple-element.12) | data formatting | bytes 33554432
  1633.7 22.6 %copy.20 = bf16[1,2048,4096]{1,2,0:T(8,128)(2,1)} copy(bf16[1,2048,4096]{2,1,0:T(8,128)(2,1)} %get-tuple-element.13) | data formatting | bytes 33554432
  1656.3 0.0 all-gather.9.cloned.1.call-update
  1656.3 0.7 pad_maximum_fusion.4
  1657.0 0.7 pad_maximum_fusion.2
  1657.7 12.1 fusion.4
  1669.8 45.2 %all-gather.7.cloned.1.call-done = bf16[256,4096]{0,1:T(8,128)(2,1)} async-done(((bf16[256,64]{0,1:T(8,128)(2,1)}), bf16[256,4096]{0,1:T(8,128)(2,1)}) %all-gather.7.cloned.1.call-update) | async-done | bytes 2097168 | tf_op jit(solution)/shard_map/all_gather | solution.py:74
  1715.0 12.5 fusion.5
  1727.5 23.0 %pad_maximum_fusion = bf16[2,2048,4096]{1,2,0:T(8,128)(2,1)} fusion(bf16[1,2048,4096]{1,2,0:T(8,128)(2,1)} %fusion.5, bf16[1,2048,4096]{1,2,0:T(8,128)(2,1)} %fusion.4), kind=kLoop, calls=%fused_computation | loop fusion | flops 16777216 | bytes 67108864 | tf_op jit(solution)/shard_map/stack | solution.py:84
  1750.5 0.0 copy-start.3
  1750.5 40.6 %copy.18 = bf16[2,2048,4096]{2,1,0:T(8,128)(2,1)} copy(bf16[2,2048,4096]{1,2,0:T(8,128)(2,1)} %pad_maximum_fusion) | data formatting | bytes 67108864
  1791.1 12.1 fusion.3
  1803.3 43.4 %all-gather.9.cloned.1.call-done = bf16[4096,256]{1,0:T(8,128)(2,1)} async-done(((bf16[64,256]{1,0:T(8,128)(2,1)}), bf16[4096,256]{1,0:T(8,128)(2,1)}) %all-gather.9.cloned.1.call-update) | async-done | bytes 2097168 | tf_op jit(solution)/shard_map/all_gather | solution.py:75
  1846.6 12.2 fusion.2
  1858.8 23.0 %pad_maximum_fusion.1 = bf16[2,4096,2048]{2,1,0:T(8,128)(2,1)} fusion(bf16[1,4096,2048]{2,1,0:T(8,128)(2,1)} %fusion.3, bf16[1,4096,2048]{2,1,0:T(8,128)(2,1)} %fusion.2), kind=kLoop, calls=%fused_computation.1 | loop fusion | flops 16777216 | bytes 67108864 | tf_op jit(solution)/shard_map/stack | solution.py:84
  (9 shorter events, 0.0 us)
Async XLA Ops:
  7.2 51.5 %all-reduce.3.cloned.1.call-start = ((), (), s32[]{:S(2)}) async-start(), calls=%async_computation.4 | async-start | bytes 4194304 | tf_op jit(solution)/shard_map/psum | solution.py:42
  29.9 41.3 %copy-start = (bf16[256,2048]{1,0:T(8,128)(2,1)S(1)}, bf16[256,2048]{1,0:T(8,128)(2,1)}, u32[]{:S(2)}) copy-start(bf16[256,2048]{1,0:T(8,128)(2,1)} %param.11) | copy-start | bytes 3145732
  29.9 118.2 %all-reduce.5.cloned.1.call-start = ((), (), s32[]{:S(2)}) async-start(), calls=%async_computation.5 | async-start | bytes 4194304 | tf_op jit(solution)/shard_map/psum | solution.py:53
  69.9 1.3 copy-start.1
  94.7 416.2 %reduce-scatter.7.cloned.1.call-start = ((), (), s32[]{:S(2)}) async-start(), calls=%async_computation.8 | async-start | bytes 4259840 | tf_op jit(solution)/shard_map/reduce_scatter | solution.py:70
  148.1 721.5 %reduce-scatter.5.cloned.1.call-start = ((), (), s32[]{:S(2)}) async-start(), calls=%async_computation.6 | async-start | bytes 4259840 | tf_op jit(solution)/shard_map/reduce_scatter | solution.py:70
  189.9 1037.8 %reduce-scatter.11.cloned.1.call-start = ((), (), s32[]{:S(2)}) async-start(), calls=%async_computation.12 | async-start | bytes 4259840 | tf_op jit(solution)/shard_map/reduce_scatter | solution.py:71
  226.2 1359.8 %reduce-scatter.9.cloned.1.call-start = ((), (), s32[]{:S(2)}) async-start(), calls=%async_computation.10 | async-start | bytes 4259840 | tf_op jit(solution)/shard_map/reduce_scatter | solution.py:71
  262.2 607.4 %copy-start.4 = (f32[2,256,64]{1,2,0:T(8,128)S(1)}, f32[2,256,64]{1,2,0:T(8,128)}, u32[]{:S(2)}) copy-start(f32[2,256,64]{1,2,0:T(8,128)} %param.16) | copy-start | bytes 393220
  262.2 607.4 %copy-start.5 = (f32[2,256,64]{1,2,0:T(8,128)S(1)}, f32[2,256,64]{1,2,0:T(8,128)}, u32[]{:S(2)}) copy-start(f32[2,256,64]{1,2,0:T(8,128)} %param.17) | copy-start | bytes 393220
  262.2 1323.7 %copy-start.6 = (f32[2,64,256]{2,1,0:T(8,128)S(1)}, f32[2,64,256]{2,1,0:T(8,128)}, u32[]{:S(2)}) copy-start(f32[2,64,256]{2,1,0:T(8,128)} %param.18) | copy-start | bytes 393220
  262.2 1323.7 %copy-start.7 = (f32[2,64,256]{2,1,0:T(8,128)S(1)}, f32[2,64,256]{2,1,0:T(8,128)}, u32[]{:S(2)}) copy-start(f32[2,64,256]{2,1,0:T(8,128)} %param.19) | copy-start | bytes 393220
  262.3 1395.5 %all-gather.5.cloned.1.call-start = ((), (), s32[]{:S(2)}) async-start(), calls=%async_computation.7 | async-start | bytes 2129920 | tf_op jit(solution)/shard_map/all_gather | solution.py:74
  871.2 843.8 %all-gather.7.cloned.1.call-start = ((), (), s32[]{:S(2)}) async-start(), calls=%async_computation.9 | async-start | bytes 2129920 | tf_op jit(solution)/shard_map/all_gather | solution.py:74
  872.0 919.2 %all-gather.11.cloned.1.call-start = ((), (), s32[]{:S(2)}) async-start(), calls=%async_computation.13 | async-start | bytes 2129920 | tf_op jit(solution)/shard_map/all_gather | solution.py:75
  1587.5 259.1 %all-gather.9.cloned.1.call-start = ((), (), s32[]{:S(2)}) async-start(), calls=%async_computation.11 | async-start | bytes 2129920 | tf_op jit(solution)/shard_map/all_gather | solution.py:75
  1633.7 24.0 %copy-start.2 = (bf16[2,2048,256]{2,1,0:T(8,128)(2,1)S(1)}, bf16[2,2048,256]{2,1,0:T(8,128)(2,1)}, u32[]{:S(2)}) copy-start(bf16[2,2048,256]{2,1,0:T(8,128)(2,1)} %param.14) | copy-start | bytes 6291460
  1750.5 40.7 %copy-start.3 = (bf16[2,2048,256]{2,1,0:T(8,128)(2,1)S(1)}, bf16[2,2048,256]{2,1,0:T(8,128)(2,1)}, u32[]{:S(2)}) copy-start(bf16[2,2048,256]{2,1,0:T(8,128)(2,1)} %param.15) | copy-start | bytes 6291460
Sparse Core Ops, SparseCore 0:
  30.1 28.5 all-reduce.2
  94.8 27.4 all-reduce.4
  148.2 362.6 reduce-scatter.6
  513.7 355.8 reduce-scatter.4
  871.8 355.8 reduce-scatter.10
  1229.9 355.9 reduce-scatter.8
  1588.8 60.3 all-gather.4
  1652.0 62.9 all-gather.6
  1717.9 62.9 all-gather.10
  1783.6 62.9 all-gather.8
where the time goes:
time: 1900 us; the launch traced here: 1890 us
  waiting for transfers between devices  1440 us (76%)
  matrix products  273 us (14%)
  local copies, waits for them, and re-layouts  111 us (6%)
  other arithmetic  50.5 us (3%)
    reduce_scatter x2, waiting for transfers between devices, local_step(): lax.psum_scatter(proj_out, 'dp', scatter_dimension=0, tiled=True)  714 us
    reduce_scatter x2, waiting for transfers between devices, local_step(): shard_in = lax.psum_scatter(proj_in, 'dp', scatter_dimension=1, tiled=True)  607 us
    dot_general x8, matrix products, contract(): lax.dot_general(left_op, right_op, (((left_dim,), (right_dim,)), ((), ())...  121 us
    dot_general x4, matrix products, contract_exact(): lax.dot_general(left_op, right_op, (((left_dim,), (right_dim,)), ((), ())...  93.9 us
    unnamed x19, local copies, waits for them, and re-layouts  87.2 us
    another operation x4, other arithmetic, local_step(): return tuple((jnp.stack(collected) for collected in results))  47.3 us
    all_gather x2, waiting for transfers between devices, local_step(): full_in = lax.all_gather(dir_in, 'dp', axis=1, tiled=True)  45.2 us
    all_gather x2, waiting for transfers between devices, local_step(): full_out = lax.all_gather(dir_out, 'dp', axis=0, tiled=True)  43.4 us
  transfers between devices with their start and end apart: 10, of which 7 were waited for; matrix products, arithmetic and copies ran while one was open for 18% of the time, Pallas kernels for 0%

commit v1 on v0

v1 whole, which is shorter than its diff:
```python
import functools

import jax
import jax.numpy as jnp
from jax import lax
from jax.experimental import pallas as pl
from jax.experimental.pallas import tpu as pltpu
from jax.sharding import PartitionSpec as P

BETA1 = 0.9
BETA2 = 0.999
EPSILON = 1e-8
STEP = 2
STEP_SIZE = 0.03 * 0.25
CORR_MOM = 1.0 - BETA1 ** STEP
CORR_VAR = 1.0 - BETA2 ** STEP

MESH = pl.DeviceIdType.MESH
BF16 = jnp.bfloat16
F32 = jnp.float32

TOK = 256
D = 2048
F = 4096
RANK = 256
DP = 64
TILE = 512
CHUNKS = 8
SLOTS = 4
DIMS = 6
COLORS = 3

CUTS = (((0, 3, 6, 8), (0, 2, 4, 8)), ((0, 3, 6, 8), (0, 3, 5, 8)))
BLOCKS = tuple(
    tuple(
        tuple((tensor, block) for tensor, cut in enumerate(cuts) for block in range(cut[color], cut[color + 1]))
        for color in range(COLORS)
    )
    for cuts in CUTS
)
WHERE = tuple(
    {item: (color, slot) for color, items in enumerate(colors) for slot, item in enumerate(items)} for colors in BLOCKS
)
FIRST_PART = tuple(CUTS[0][0][color + 1] - CUTS[0][0][color] for color in range(COLORS))


def ring_bits(position):
    high = lax.div(position, 2)
    return [lax.rem(high + position, 2), high]


def device_bits(dp):
    return ring_bits(lax.rem(dp, 4)) + ring_bits(lax.rem(lax.div(dp, 4), 4)) + ring_bits(lax.div(dp, 16))


def step_bits(tile, lane):
    x = lane % 4
    odd = lax.rem(tile, 2)
    y_low = odd if lane < 4 else 1 - odd
    z_high = lax.div(tile, 4)
    z_low = lax.rem(z_high + lax.rem(lax.div(tile, 2), 2), 2)
    return [(x // 2 + x) % 2, x // 2, y_low, odd, z_low, z_high]


def stage_dim(color, stage, core):
    return (2 * color + core + stage) % DIMS


def place(bits, color, tp):
    at = [sum(bits[stage_dim(color, stage, core)] * (32 >> stage) for stage in range(DIMS)) for core in range(2)]
    return at[0] * (1 - tp) + at[1] * tp


def flip(dp, dim):
    stride = 4 ** (dim // 2)
    position = lax.rem(lax.div(dp, stride), 4)
    other = 3 - position if dim % 2 else position + 1 - 2 * lax.rem(position, 2)
    return dp + (other - position) * stride


def by_core(tp, function, color, stage):
    zero, one = (function(stage_dim(color, stage, core)) for core in range(2))
    return zero * (1 - tp) + one * tp


def dot(left, right, left_dim=1, right_dim=0):
    return lax.dot_general(left, right, (((left_dim,), (right_dim,)), ((), ())), preferred_element_type=F32)


GELU_A = 0.7978845608028654
GELU_B = 0.044715


def gelu(z):
    return 0.5 * z * (1.0 + jnp.tanh(GELU_A * (z + GELU_B * z * z * z)))


def gelu_grad(z):
    square = z * z
    t = jnp.tanh(GELU_A * (z + GELU_B * z * square))
    return 0.5 * (1.0 + t) + 0.5 * z * (1.0 - t * t) * (GELU_A * (1.0 + 3.0 * GELU_B * square))


def step_kernel(x_hbm, g_hbm, w_in, w_out, p_in, q_out, m_ref, v_ref, *rest):
    rest = iter(rest)

    def by_group():
        return tuple(tuple(next(rest) for color in range(COLORS)) for group in range(2))

    n_out = by_group()
    m_new, v_new = next(rest), next(rest)
    red, got, gat = by_group(), by_group(), by_group()
    (h_buf, g_buf, a_buf, z0_buf, z1_buf, w_buf, pq_buf, hp0, gq1, hp1, gq0,
     w_sem, in_sem, pq_sem, out_sem, pair_send, pair_recv, send_sem, recv_sem) = rest
    dp = lax.axis_index("dp")
    tp = lax.axis_index("tp")
    bits = device_bits(dp)

    barrier = pltpu.get_barrier_semaphore()
    for dim in range(DIMS):
        pl.semaphore_signal(barrier, inc=1, device_id={"dp": flip(dp, dim)}, device_id_type=MESH)
    pl.semaphore_signal(barrier, inc=1, device_id={"tp": 1 - tp}, device_id_type=MESH)
    pl.semaphore_wait(barrier, DIMS + 1)

    def block_of(phase, chunk, q):
        name, layer = phase
        half, rest_ = lax.rem(chunk, 2), lax.div(chunk, 2)
        if name == "z":
            return w_in.at[layer, pl.ds(TILE * q, TILE), pl.ds(pl.multiple_of(TILE * chunk, TILE), TILE)]
        if name == "h":
            return w_out.at[layer, pl.ds(pl.multiple_of(2048 * half, TILE) + TILE * q, TILE),
                            pl.ds(pl.multiple_of(TILE * rest_, TILE), TILE)]
        if name == "da":
            return w_out.at[layer, pl.ds(pl.multiple_of(TILE * chunk, TILE), TILE), pl.ds(TILE * q, TILE)]
        return w_in.at[layer, pl.ds(pl.multiple_of(TILE * rest_, TILE), TILE),
                       pl.ds(pl.multiple_of(2048 * half + TILE * q, TILE), TILE)]

    def start_chunk(phase, chunk):
        slot = lax.rem(chunk, SLOTS)
        for q in range(4):
            pltpu.make_async_copy(block_of(phase, chunk, q), w_buf.at[slot, q], w_sem.at[slot]).start()

    def wait_chunk(chunk):
        slot = lax.rem(chunk, SLOTS)
        pltpu.make_async_copy(w_buf.at[slot], w_buf.at[slot], w_sem.at[slot]).wait()
        return slot

    phases = (("z", 0), ("h", 0), ("z", 1), ("da", 1), ("b", 1), ("da", 0))

    def take_chunk(index, chunk):
        ahead = chunk + SLOTS - 1

        @pl.when(ahead < CHUNKS)
        def _():
            start_chunk(phases[index], ahead)

        if index + 1 < len(phases):

            @pl.when(ahead >= CHUNKS)
            def _():
                start_chunk(phases[index + 1], ahead - CHUNKS)

        return wait_chunk(chunk)

    def load_pq(ref, layer, slot):
        pltpu.make_async_copy(ref.at[layer], pq_buf.at[slot], pq_sem.at[slot]).start()

    def wait_pq(ref, slot):
        pltpu.make_async_copy(ref.at[0], pq_buf.at[slot], pq_sem.at[slot]).wait()

    x_copy = pltpu.make_async_copy(x_hbm, h_buf, in_sem.at[0])
    g_copy = pltpu.make_async_copy(g_hbm, g_buf, in_sem.at[1])
    x_copy.start()
    for chunk in range(SLOTS - 1):
        start_chunk(phases[0], jnp.int32(chunk))
    g_copy.start()
    load_pq(p_in, 0, 0)
    load_pq(q_out, 1, 1)

    def split(values, out_ref):
        high = values.astype(BF16)
        rest_ = values - high.astype(F32)
        middle = rest_.astype(BF16)
        low = (rest_ - middle.astype(F32)).astype(BF16)
        out_ref[:, 0:RANK] = high
        out_ref[:, RANK : 2 * RANK] = middle
        out_ref[:, 2 * RANK : 3 * RANK] = low

    def project(rows, parts, group, tensor, tile):
        wide = dot(rows, parts[...], 0, 0)
        total = wide[:, 2 * RANK : 3 * RANK] + wide[:, RANK : 2 * RANK] + wide[:, 0:RANK]
        for lane in range(8):
            lane_bits = step_bits(tile, lane)
            spots = [place(lane_bits, color, tp) for color in range(COLORS)]
            for block in range(8):
                color, slot = WHERE[group][tensor, block]
                row, col = 64 * lane + 16 * (block // 2), 128 * (block % 2)
                red[group][color][slot, spots[color]] = total[row : row + 16, col : col + 128]

    def columns(tile):
        return pl.ds(pl.multiple_of(TILE * tile, TILE), TILE)

    def pair_copy(exchange, n):
        return pltpu.make_async_remote_copy(
            src_ref=red[1][0].at[n], dst_ref=red[1][1 + exchange].at[n],
            send_sem=pair_send.at[exchange, n], recv_sem=pair_recv.at[exchange, n],
            device_id={"tp": 1 - tp}, device_id_type=MESH)

    def pair_send_tile(exchange, n, values):
        for a in range(16):
            for b in range(4):
                red[1][0][n, 4 * a + b] = values[16 * a : 16 * a + 16, 128 * b : 128 * b + 128]
        pair_copy(exchange, n).start()

    def pair_add(exchange, state):
        def one(n, carry):
            pair_copy(exchange, n).wait()
            for a in range(16):
                for b in range(4):
                    cols = pl.ds(pl.multiple_of(TILE * n + 128 * b, 128), 128)
                    both = red[1][0][n, 4 * a + b] + red[1][1 + exchange][n, 4 * a + b]
                    state[16 * a : 16 * a + 16, cols] = (
                        state[16 * a : 16 * a + 16, cols].astype(F32) + both).astype(BF16)
            return carry

        lax.fori_loop(0, 4, one, 0)

    own = [place(bits, color, tp) for color in range(COLORS)]

    def message(group, color, number, source, target, dim_stage):
        return pltpu.make_async_remote_copy(
            src_ref=source, dst_ref=target,
            send_sem=send_sem.at[group, color, number], recv_sem=recv_sem.at[group, color, number],
            device_id={"dp": by_core(tp, functools.partial(flip, dp), color, dim_stage)}, device_id_type=MESH)

    def start_of(color, stage):
        width = DP >> stage
        return lax.div(own[color], width) * width

    def reduce_copy(group, color, stage, part, parts, slots=None):
        half = 32 >> stage
        size = half // parts
        mine = lax.rem(lax.div(own[color], half), 2)
        source = start_of(color, stage) + (1 - mine) * half + part * size
        target = DP - (DP >> stage) + part * size
        slots = slice(None) if slots is None else slots
        number = (part if slots == slice(None) else (0 if slots.start == 0 else 1)) if stage == 0 else (
            4 + part if stage == 1 else 4 + stage)
        return message(group, color, number, red[group][color].at[slots, pl.ds(source, size)],
                       got[group][color].at[slots, pl.ds(target, size)], stage)

    def reduce_part(group, color, stage, part, parts):
        if group == 0 and stage == 0:
            first = FIRST_PART[color]
            return reduce_copy(group, color, 0, 0, 1, slice(first, len(BLOCKS[0][color])) if part else slice(0, first))
        return reduce_copy(group, color, stage, part, parts)

    def reduce_send(group, stage, parts=1, part=0):
        for color in range(COLORS):
            reduce_part(group, color, stage, part, parts).start()

    def reduce_add(group, stage, parts=1):
        half = 32 >> stage
        step = min(half, 4)
        for color in range(COLORS):
            for part in range(2 if group == 0 and stage == 0 else parts):
                reduce_part(group, color, stage, part, parts).wait()
            kept = start_of(color, stage + 1)
            offset = DP - (DP >> stage)

            def one(i, carry):
                for slot in range(len(BLOCKS[group][color])):
                    to = pl.ds(kept + step * i, step)
                    red[group][color][slot, to] = (
                        red[group][color][slot, to] + got[group][color][slot, pl.ds(offset + step * i, step)])
                return carry

            lax.fori_loop(0, half // step, one, 0)

    def update(group):
        for color in range(COLORS):
            for slot, (tensor, block) in enumerate(BLOCKS[group][color]):
                row, col = 16 * (block // 2), 128 * (block % 2)
                spot = (2 * group + tensor, slice(row, row + 16), slice(col, col + 128))
                grad = red[group][color][slot, own[color]]
                moment = BETA1 * m_ref[spot] + (1.0 - BETA1) * grad
                second = BETA2 * v_ref[spot] + (1.0 - BETA2) * grad * grad
                m_new[spot] = moment
                v_new[spot] = second
                direction = (moment / CORR_MOM) / (jnp.sqrt(second / CORR_VAR) + EPSILON)
                gat[group][color][slot, own[color]] = direction.astype(BF16)

    def gather_copy(group, color, turn, part, parts):
        stage = DIMS - 1 - turn
        size = (1 << turn) // parts
        spot = pl.ds(start_of(color, stage + 1) + part * size, size)
        number = 10 + turn + part
        return message(group, color, number, gat[group][color].at[:, spot], gat[group][color].at[:, spot], stage)

    def gather_send(group, turn, parts=1, part=0):
        for color in range(COLORS):
            gather_copy(group, color, turn, part, parts).start()

    def gather_wait(group, turn, parts=1):
        for color in range(COLORS):
            for part in range(parts):
                gather_copy(group, color, turn, part, parts).wait()

    def write_out(group, wait=False):
        for color in range(COLORS):
            copy = pltpu.make_async_copy(gat[group][color], n_out[group][color], out_sem.at[group, color])
            copy.wait() if wait else copy.start()

    x_copy.wait()

    def z0_step(tile, carry):
        slot = take_chunk(0, tile)
        z = sum(dot(h_buf[:, TILE * q : TILE * (q + 1)], w_buf[slot, q]) for q in range(4)).astype(BF16)
        z0_buf[:, columns(tile)] = z
        a_buf[:, columns(tile)] = gelu(z.astype(F32)).astype(BF16)
        return carry

    lax.fori_loop(0, CHUNKS, z0_step, 0)

    def h_step(n, carry):
        total = None
        for half in range(2):
            slot = take_chunk(1, 2 * n + half)
            for q in range(4):
                at = 2048 * half + TILE * q
                term = dot(a_buf[:, at : at + TILE], w_buf[slot, q])
                total = term if total is None else total + term
        pair_send_tile(0, n, total)
        return carry

    lax.fori_loop(0, 4, h_step, 0)
    wait_pq(p_in, 0)
    split(dot(h_buf[...], pq_buf[0]), hp0)
    load_pq(p_in, 1, 0)
    g_copy.wait()
    wait_pq(q_out, 1)
    split(dot(g_buf[...], pq_buf[1]), gq1)
    load_pq(q_out, 0, 1)
    pair_add(0, h_buf)

    def z1_step(tile, carry):
        slot = take_chunk(2, tile)
        z = sum(dot(h_buf[:, TILE * q : TILE * (q + 1)], w_buf[slot, q]) for q in range(4)).astype(BF16)
        z1_buf[:, columns(tile)] = z
        project(gelu(z.astype(F32)).astype(BF16), gq1, 0, 0, tile)
        return carry

    lax.fori_loop(0, CHUNKS, z1_step, 0)
    reduce_send(0, 0, part=0)
    wait_pq(p_in, 0)
    split(dot(h_buf[...], pq_buf[0]), hp1)

    def da1_step(tile, carry):
        slot = take_chunk(3, tile)
        d_act = sum(dot(g_buf[:, TILE * q : TILE * (q + 1)], w_buf[slot, q], 1, 1) for q in range(4))
        dz = (gelu_grad(z1_buf[:, columns(tile)].astype(F32)) * d_act).astype(BF16)
        z1_buf[:, columns(tile)] = dz
        project(dz, hp1, 0, 1, tile)
        return carry

    lax.fori_loop(0, CHUNKS, da1_step, 0)
    reduce_send(0, 0, part=1)

    def b_step(n, carry):
        total = None
        for half in range(2):
            slot = take_chunk(4, 2 * n + half)
            for q in range(4):
                at = 2048 * half + TILE * q
                term = dot(z1_buf[:, at : at + TILE], w_buf[slot, q], 1, 1)
                total = term if total is None else total + term
        pair_send_tile(1, n, total)
        return carry

    lax.fori_loop(0, 4, b_step, 0)
    wait_pq(q_out, 1)
    pair_add(1, g_buf)
    split(dot(g_buf[...], pq_buf[1]), gq0)

    def da0_step(tile, carry):
        slot = take_chunk(5, tile)
        project(a_buf[:, columns(tile)], gq0, 1, 0, tile)
        d_act = sum(dot(g_buf[:, TILE * q : TILE * (q + 1)], w_buf[slot, q], 1, 1) for q in range(4))
        dz = (gelu_grad(z0_buf[:, columns(tile)].astype(F32)) * d_act).astype(BF16)
        project(dz, hp0, 1, 1, tile)
        return carry

    lax.fori_loop(0, CHUNKS, da0_step, 0)

    for stage in range(4):
        reduce_add(0, stage)
        reduce_send(0, stage + 1)
        reduce_send(1, 0, 4, stage)
    reduce_add(0, 4)
    reduce_send(0, 5)
    reduce_add(1, 0, 4)
    reduce_send(1, 1, 2, 0)
    reduce_add(0, 5)
    update(0)
    gather_send(0, 0)
    reduce_send(1, 1, 2, 1)
    gather_wait(0, 0)
    gather_send(0, 1)
    for stage in range(1, 5):
        reduce_add(1, stage, 2 if stage == 1 else 1)
        reduce_send(1, stage + 1)
        gather_wait(0, stage)
        if stage < 4:
            gather_send(0, stage + 1)
    gather_send(0, 5, 4, 0)
    reduce_add(1, 5)
    update(1)
    gather_send(1, 0)
    gather_send(0, 5, 4, 1)
    for turn in range(2):
        gather_wait(1, turn)
        gather_send(1, turn + 1)
        gather_send(0, 5, 4, 2 + turn)
    for turn in range(2, 5):
        gather_wait(1, turn)
        gather_send(1, turn + 1)
        if turn == 3:
            gather_wait(0, 5, 4)
            write_out(0)
    gather_wait(1, 5)
    write_out(1)
    write_out(0, wait=True)
    write_out(1, wait=True)


def apply_kernel(order, w_in, w_out, p_in, q_out, *rest):
    gat = (rest[0:3], rest[3:6])
    in_new, out_new, n_buf = rest[6:9]
    layer = order - 1 - pl.program_id(0)
    tile = pl.program_id(1)
    tp = lax.axis_index("tp")
    for group in range(2):

        @pl.when(layer == 1 - group)
        def _():
            for lane in range(8):
                lane_bits = step_bits(tile, lane)
                spots = [place(lane_bits, color, tp) for color in range(COLORS)]
                for tensor in range(2):
                    for block in range(8):
                        color, slot = WHERE[group][tensor, block]
                        row, col = 64 * lane + 16 * (block // 2), 128 * (block % 2)
                        n_buf[tensor, row : row + 16, col : col + 128] = gat[group][color][slot, spots[color]]

    for cut in range(4):
        cols = slice(512 * cut, 512 * (cut + 1))
        change = dot(n_buf[0], q_out[0, cols, :], 1, 1)
        out_new[0, :, cols] = (w_out[0, :, cols].astype(F32) - STEP_SIZE * change).astype(BF16)
        change = dot(p_in[0, cols, :], n_buf[1], 1, 1)
        in_new[0, cols, :] = (w_in[0, cols, :].astype(F32) - STEP_SIZE * change).astype(BF16)


def local_step(x_rows, g_rows, w_in, w_out, p_in, q_out, m_in, v_in, m_out, v_out):
    def gathered(outs, ins):
        return jnp.stack([outs[1], ins[1].T, outs[0], ins[0].T])

    any_spec = pl.BlockSpec(memory_space=pl.ANY)
    vmem_spec = pl.BlockSpec(memory_space=pltpu.VMEM)
    shares = [jax.ShapeDtypeStruct((len(items), DP, 16, 128), BF16) for colors in BLOCKS for items in colors]
    moments = jax.ShapeDtypeStruct((4, 64, RANK), F32)
    results = pl.pallas_call(
        step_kernel,
        out_shape=shares + [moments, moments],
        in_specs=[any_spec] * 6 + [vmem_spec] * 2,
        out_specs=[any_spec] * 6 + [vmem_spec] * 2,
        scratch_shapes=[pltpu.VMEM(s.shape, F32) for s in shares]
        + [pltpu.VMEM((s.shape[0], DP - 1, 16, 128), F32) for s in shares]
        + [pltpu.VMEM(s.shape, BF16) for s in shares]
        + [
            pltpu.VMEM((TOK, D), BF16),
            pltpu.VMEM((TOK, D), BF16),
            pltpu.VMEM((TOK, F), BF16),
            pltpu.VMEM((TOK, F), BF16),
            pltpu.VMEM((TOK, F), BF16),
            pltpu.VMEM((SLOTS, 4, TILE, TILE), BF16),
            pltpu.VMEM((2, D, RANK), BF16),
            pltpu.VMEM((TOK, 3 * RANK), BF16),
            pltpu.VMEM((TOK, 3 * RANK), BF16),
            pltpu.VMEM((TOK, 3 * RANK), BF16),
            pltpu.VMEM((TOK, 3 * RANK), BF16),
            pltpu.SemaphoreType.DMA((SLOTS,)),
            pltpu.SemaphoreType.DMA((2,)),
            pltpu.SemaphoreType.DMA((2,)),
            pltpu.SemaphoreType.DMA((2, 3)),
            pltpu.SemaphoreType.DMA((2, 4)),
            pltpu.SemaphoreType.DMA((2, 4)),
            pltpu.SemaphoreType.DMA((2, 3, 20)),
            pltpu.SemaphoreType.DMA((2, 3, 20)),
        ],
        compiler_params=pltpu.CompilerParams(
            collective_id=0, has_side_effects=True, vmem_limit_bytes=67_000_000),
        name="galore_step",
    )(x_rows, g_rows, w_in, w_out, p_in, q_out, gathered(m_out, m_in), gathered(v_out, v_in))
    shares_new, (m_new, v_new) = results[:6], results[6:]

    layers = w_in.shape[0]
    in_block = pl.BlockSpec((1, D, TILE), lambda i, j: (layers - 1 - i, 0, j))
    out_block = pl.BlockSpec((1, TILE, D), lambda i, j: (layers - 1 - i, j, 0))
    basis = pl.BlockSpec((1, D, RANK), lambda i, j: (layers - 1 - i, 0, 0))
    w_in_new, w_out_new = pl.pallas_call(
        functools.partial(apply_kernel, layers),
        grid=(layers, F // TILE),
        out_shape=[jax.ShapeDtypeStruct(w_in.shape, BF16), jax.ShapeDtypeStruct(w_out.shape, BF16)],
        in_specs=[in_block, out_block, basis, basis] + [vmem_spec] * 6,
        out_specs=[in_block, out_block],
        scratch_shapes=[pltpu.VMEM((2, TILE, RANK), BF16)],
        compiler_params=pltpu.CompilerParams(vmem_limit_bytes=60_000_000),
        name="galore_apply",
    )(w_in, w_out, p_in, q_out, *shares_new)

    def split_moments(values):
        return jnp.stack([values[3].T, values[1].T]), jnp.stack([values[2], values[0]])

    m_in_new, m_out_new = split_moments(m_new)
    v_in_new, v_out_new = split_moments(v_new)
    return w_in_new, w_out_new, m_in_new, v_in_new, m_out_new, v_out_new


def solution(mesh):
    weight_in_spec = P(None, None, "tp")
    weight_out_spec = P(None, "tp", None)
    moment_in_spec = P(None, None, ("tp", "dp"))
    moment_out_spec = P(None, ("tp", "dp"), None)
    return jax.shard_map(
        local_step,
        mesh=mesh,
        in_specs=(P("dp", None), P("dp", None), weight_in_spec, weight_out_spec, P(), P(),
                  moment_in_spec, moment_in_spec, moment_out_spec, moment_out_spec),
        out_specs=(weight_in_spec, weight_out_spec, moment_in_spec, moment_in_spec, moment_out_spec, moment_out_spec),
        check_vma=False,
    )
```

time: 1900 us -> 250 us (0.13)
  waiting for transfers between devices: 1440 us -> 0 us
  matrix products: 273 us -> 0 us
  Pallas kernels: 0 us -> 239 us
  local copies, waits for them, and re-layouts: 111 us -> 4.63 us
  other arithmetic: 50.5 us -> 4.1 us
    reduce_scatter x4 -> x0, waiting for transfers between devices: 1320 us -> none  [the longest x2 714 us: local_step(): lax.psum_scatter(proj_out, 'dp', scatter_dimension=0, tiled=True)]
    dot_general x17 -> x0, matrix products: 273 us -> none  [the longest x8 121 us: contract(): lax.dot_general(left_op, right_op, (((left_dim,), (right_dim,)), ((), ())...]
    pallas_call x0 -> x2, Pallas kernels: none -> 239 us  [the longest x1 183 us: local_step(): pl.pallas_call(step_kernel, out_shape=shares + [moments, moments], in_spe...]
    all_gather x4 -> x0, waiting for transfers between devices: 88.5 us -> none  [the longest x2 45.2 us: local_step(): full_in = lax.all_gather(dir_in, 'dp', axis=1, tiled=True)]
    unnamed x19 -> x0, local copies, waits for them, and re-layouts: 87.2 us -> none
    another operation x4 -> x6, other arithmetic: 47.3 us -> 4.1 us  [the longest x2 1.45 us: gathered(): return jnp.stack([outs[1], ins[1].T, outs[0], ins[0].T])]
    psum x2 -> x0, waiting for transfers between devices: 28.2 us -> none  [the longest x1 28.2 us: forward_backward(): lax.psum(jnp.dot(act_bf16, w_out[layer_idx], preferred_element_type=jnp.f...]
    slice x1 -> x3, local copies, waits for them, and re-layouts: 23.4 us -> 2.87 us  [the longest x2 1.76 us: gathered(): return jnp.stack([outs[1], ins[1].T, outs[0], ins[0].T])]
  transfers between devices with their start and end apart: 10 -> 0, of which waited for: 7 -> 0; matrix products, arithmetic and copies ran while one was open for 18% -> 0% of each run, Pallas kernels for 0% -> 0%
where the time goes in v1:
time: 250 us; the launch traced here: 248 us
  Pallas kernels  239 us (96%)
  local copies, waits for them, and re-layouts  4.63 us (2%)
  other arithmetic  4.1 us (2%)
    pallas_call x1, Pallas kernels, local_step(): pl.pallas_call(step_kernel, out_shape=shares + [moments, moments], in_spe...  183 us
    pallas_call x1, Pallas kernels, local_step(): pl.pallas_call(functools.partial(apply_kernel, layers), grid=(layers, F /...  56 us

profile of v1, /device:TPU:0, one launch (start us, length us, event | category | flops | bytes accessed | tf_op | source)
XLA Modules:
  0.0 248.4 jit_solution(4548055652083194531)
XLA Ops:
  0.6 0.9 slice_bitcast_fusion.7
  1.5 0.9 slice_bitcast_fusion.5
  2.4 0.9 fusion.3
  3.3 0.7 pad_maximum_fusion.m_ref
  4.0 0.9 fusion.2
  4.9 0.7 pad_maximum_fusion.1.v_ref
  5.6 182.9 %galore_step.1 = (bf16[5,64,16,128]{3,2,1,0:T(8,128)(2,1)}, bf16[5,64,16,128]{3,2,1,0:T(8,128)(2,1)}, bf16[6,64,16,128]{3,2,1,0:T(8,128)(2,1)}, bf16[6,64,16,128...) custom-call(bf16[256,2048]{1,0:T(8,128)(2,1)} %x_hbm.1, ...), custom_call_target="tpu_custom_call" | custom-call | tf_op jit(solution)/shard_map/galore_step/pallas_call | solution.py:471
  188.6 1.1 fusion
  189.7 0.7 pad_maximum_fusion.5
  190.3 0.7 pad_maximum_fusion.3
  191.0 0.7 pad_maximum_fusion.2
  191.7 0.7 pad_maximum_fusion.4
  192.3 56.0 %galore_apply.1 = (bf16[2,2048,4096]{2,1,0:T(8,128)(2,1)}, bf16[2,4096,2048]{2,1,0:T(8,128)(2,1)}) custom-call(bf16[2,2048,4096]{2,1,0:T(8,128)(2,1)} %w_in.3, bf16[2,4096,2048]{2,1,0:T(8,128)(2,1)} %w_out.3, bf16[2,2048,256]{2,1,0:T(8,128)(2,1)} %p_in.3, bf16[2,2048,256]{2,1,0:T(8,128)(2,1)} %q_out.3, bf16[5,64,16,128]{3,2,1,0:T(8,128)(2,1)} %get-tuple-element.16.rest_0_, ...), custom_call_target="tpu_custom_call" | custom-call | tf_op jit(solution)/shard_map/galore_apply/pallas_call | solution.py:510

commit v2 on v1

v2 whole, which is shorter than its diff:
```python
import functools

import jax
import jax.numpy as jnp
from jax import lax
from jax.experimental import pallas as pl
from jax.experimental.pallas import tpu as pltpu
from jax.sharding import PartitionSpec as P

BETA1 = 0.9
BETA2 = 0.999
EPSILON = 1e-8
STEP = 2
STEP_SIZE = 0.03 * 0.25
CORR_MOM = 1.0 - BETA1 ** STEP
CORR_VAR = 1.0 - BETA2 ** STEP

MESH = pl.DeviceIdType.MESH
BF16 = jnp.bfloat16
F32 = jnp.float32

TOK = 256
D = 2048
F = 4096
RANK = 256
DP = 64
TILE = 512
QUARTERS = range(4)
CHUNKS = 8
SLOTS = 4
DIMS = 6
COLORS = 3

CUTS = (((0, 3, 6, 8), (0, 2, 4, 8)), ((0, 3, 6, 8), (0, 3, 5, 8)))
BLOCKS = tuple(
    tuple(
        tuple((tensor, block) for tensor, cut in enumerate(cuts) for block in range(cut[color], cut[color + 1]))
        for color in range(COLORS)
    )
    for cuts in CUTS
)
WHERE = tuple(
    {item: (color, slot) for color, items in enumerate(colors) for slot, item in enumerate(items)} for colors in BLOCKS
)
FIRST_PART = tuple(CUTS[0][0][color + 1] - CUTS[0][0][color] for color in range(COLORS))


def ring_bits(position):
    high = lax.div(position, 2)
    return [lax.rem(high + position, 2), high]


def device_bits(dp):
    return ring_bits(lax.rem(dp, 4)) + ring_bits(lax.rem(lax.div(dp, 4), 4)) + ring_bits(lax.div(dp, 16))


def step_bits(tile, lane):
    x = lane % 4
    odd = lax.rem(tile, 2)
    y_low = odd if lane < 4 else 1 - odd
    z_high = lax.div(tile, 4)
    z_low = lax.rem(z_high + lax.rem(lax.div(tile, 2), 2), 2)
    return [(x // 2 + x) % 2, x // 2, y_low, odd, z_low, z_high]


def stage_dim(color, stage, core):
    return (2 * color + core + stage) % DIMS


def place(bits, color, tp):
    at = [sum(bits[stage_dim(color, stage, core)] * (32 >> stage) for stage in range(DIMS)) for core in range(2)]
    return at[0] * (1 - tp) + at[1] * tp


def flip(dp, dim):
    stride = 4 ** (dim // 2)
    position = lax.rem(lax.div(dp, stride), 4)
    other = 3 - position if dim % 2 else position + 1 - 2 * lax.rem(position, 2)
    return dp + (other - position) * stride


def by_core(tp, function, color, stage):
    zero, one = (function(stage_dim(color, stage, core)) for core in range(2))
    return zero * (1 - tp) + one * tp


def dot(left, right, left_dim=1, right_dim=0):
    return lax.dot_general(left, right, (((left_dim,), (right_dim,)), ((), ())), preferred_element_type=F32)


GELU_A = 0.7978845608028654
GELU_B = 0.044715


def gelu(z):
    return 0.5 * z * (1.0 + jnp.tanh(GELU_A * (z + GELU_B * z * z * z)))


def gelu_grad(z):
    square = z * z
    t = jnp.tanh(GELU_A * (z + GELU_B * z * square))
    return 0.5 * (1.0 + t) + 0.5 * z * (1.0 - t * t) * (GELU_A * (1.0 + 3.0 * GELU_B * square))


def step_kernel(x_hbm, g_hbm, w_in, w_out, p_in, q_out, m_in, v_in, m_out, v_out, *rest):
    rest = iter(rest)

    def by_group():
        return tuple(tuple(next(rest) for color in range(COLORS)) for group in range(2))

    n_out = by_group()
    m_new, v_new = next(rest), next(rest)
    red, got, gat = by_group(), by_group(), by_group()
    (h_buf, g_buf, a_buf, z0_buf, z1_buf, w_buf, pq_buf, hp0, gq1, hp1, gq0,
     w_sem, in_sem, pq_sem, out_sem, pair_send, pair_recv, send_sem, recv_sem) = rest
    dp = lax.axis_index("dp")
    tp = lax.axis_index("tp")
    bits = device_bits(dp)

    def direct_device(color, mask):
        ends = []
        for core in range(2):
            end = dp
            for stage in range(3, DIMS):
                if mask & (32 >> stage):
                    end = flip(end, stage_dim(color, stage, core))
            ends.append(end)
        return ends[0] * (1 - tp) + ends[1] * tp

    barrier = pltpu.get_barrier_semaphore()
    greeted = set()
    for color in range(COLORS):
        for mask in range(1, 8):
            dims = tuple(
                tuple(sorted(stage_dim(color, stage, core) for stage in range(3, DIMS) if mask & (32 >> stage)))
                for core in range(2))
            if dims not in greeted:
                greeted.add(dims)
                pl.semaphore_signal(barrier, device_id={"dp": direct_device(color, mask)}, device_id_type=MESH)
    pl.semaphore_signal(barrier, device_id={"tp": 1 - tp}, device_id_type=MESH)
    pl.semaphore_wait(barrier, len(greeted) + 1)

    def block_of(phase, chunk, q):
        name, layer = phase
        half, rest_ = lax.rem(chunk, 2), lax.div(chunk, 2)
        if name == "z":
            return w_in.at[layer, pl.ds(TILE * q, TILE), pl.ds(pl.multiple_of(TILE * chunk, TILE), TILE)]
        if name == "h":
            return w_out.at[layer, pl.ds(pl.multiple_of(2048 * half, TILE) + TILE * q, TILE),
                            pl.ds(pl.multiple_of(TILE * rest_, TILE), TILE)]
        if name == "da":
            return w_out.at[layer, pl.ds(pl.multiple_of(TILE * chunk, TILE), TILE), pl.ds(TILE * q, TILE)]
        return w_in.at[layer, pl.ds(pl.multiple_of(TILE * rest_, TILE), TILE),
                       pl.ds(pl.multiple_of(2048 * half + TILE * q, TILE), TILE)]

    def start_chunk(phase, chunk):
        slot = lax.rem(chunk, SLOTS)
        for q in QUARTERS:
            pltpu.make_async_copy(block_of(phase, chunk, q), w_buf.at[slot, q], w_sem.at[slot]).start()

    def wait_chunk(chunk):
        slot = lax.rem(chunk, SLOTS)
        pltpu.make_async_copy(w_buf.at[slot], w_buf.at[slot], w_sem.at[slot]).wait()
        return slot

    phases = (("z", 0), ("h", 0), ("z", 1), ("da", 1), ("b", 1), ("da", 0))

    def take_chunk(index, chunk):
        ahead = chunk + SLOTS - 1

        @pl.when(ahead < CHUNKS)
        def _():
            start_chunk(phases[index], ahead)

        if index + 1 < len(phases):

            @pl.when(ahead >= CHUNKS)
            def _():
                start_chunk(phases[index + 1], ahead - CHUNKS)

        return wait_chunk(chunk)

    def load_pq(ref, layer, slot):
        pltpu.make_async_copy(ref.at[layer], pq_buf.at[slot], pq_sem.at[slot]).start()

    def wait_pq(ref, slot):
        pltpu.make_async_copy(ref.at[0], pq_buf.at[slot], pq_sem.at[slot]).wait()

    x_copy = pltpu.make_async_copy(x_hbm, h_buf, in_sem.at[0])
    g_copy = pltpu.make_async_copy(g_hbm, g_buf, in_sem.at[1])
    x_copy.start()
    for chunk in range(SLOTS - 1):
        start_chunk(phases[0], jnp.int32(chunk))
    g_copy.start()
    load_pq(p_in, 0, 0)
    load_pq(q_out, 1, 1)

    def split(values, out_ref):
        for part in range(3):
            piece = values.astype(BF16)
            out_ref[:, RANK * part : RANK * (part + 1)] = piece
            values = values - piece.astype(F32)

    def project(rows, parts, group, tensor, tile):
        wide = dot(rows, parts[...], 0, 0)
        total = wide[:, 2 * RANK : 3 * RANK] + wide[:, RANK : 2 * RANK] + wide[:, 0:RANK]
        for lane in range(8):
            lane_bits = step_bits(tile, lane)
            spots = [place(lane_bits, color, tp) for color in range(COLORS)]
            for block in range(8):
                color, slot = WHERE[group][tensor, block]
                row, col = 64 * lane + 16 * (block // 2), 128 * (block % 2)
                red[group][color][slot, spots[color]] = total[row : row + 16, col : col + 128]

    def columns(tile):
        return pl.ds(pl.multiple_of(TILE * tile, TILE), TILE)

    def pair_copy(exchange, n):
        return pltpu.make_async_remote_copy(
            src_ref=red[1][0].at[n], dst_ref=red[1][1 + exchange].at[n],
            send_sem=pair_send.at[exchange, n], recv_sem=pair_recv.at[exchange, n],
            device_id={"tp": 1 - tp}, device_id_type=MESH)

    def pair_send_tile(exchange, n, values):
        for a in range(16):
            for b in QUARTERS:
                red[1][0][n, 4 * a + b] = values[16 * a : 16 * a + 16, 128 * b : 128 * b + 128]
        pair_copy(exchange, n).start()

    def pair_add(exchange, state):
        def one(n, carry):
            pair_copy(exchange, n).wait()
            for a in range(16):
                for b in QUARTERS:
                    cols = pl.ds(pl.multiple_of(TILE * n + 128 * b, 128), 128)
                    both = red[1][0][n, 4 * a + b] + red[1][1 + exchange][n, 4 * a + b]
                    state[16 * a : 16 * a + 16, cols] = (
                        state[16 * a : 16 * a + 16, cols].astype(F32) + both).astype(BF16)
            return carry

        lax.fori_loop(0, 4, one, 0)

    own = [place(bits, color, tp) for color in range(COLORS)]

    def message(group, color, number, source, target, device):
        return pltpu.make_async_remote_copy(
            src_ref=source, dst_ref=target,
            send_sem=send_sem.at[group, color, number], recv_sem=recv_sem.at[group, color, number],
            device_id={"dp": device}, device_id_type=MESH)

    def start_of(color, stage):
        width = DP >> stage
        return lax.div(own[color], width) * width

    def bit(color, stage):
        return lax.rem(lax.div(own[color], 32 >> stage), 2)

    def cut(group, color, stage, part):
        half = 32 >> stage
        every = slice(0, len(BLOCKS[group][color]))
        if stage == 2:
            return every, 0, 0, half
        if group == 0 and stage == 0:
            first = FIRST_PART[color]
            return (slice(first, every.stop) if part else slice(0, first)), 0, 0, half
        ahead = bit(color, stage + 1)
        quarter = half // 2
        return every, (ahead if part else 1 - ahead) * quarter, part * quarter, quarter

    def reduce_copy(group, color, stage, part):
        slots, offset, into, size = cut(group, color, stage, part)
        source = start_of(color, stage) + (1 - bit(color, stage)) * (32 >> stage) + offset
        target = DP - (DP >> stage) + into
        return message(group, color, 2 * stage + part, red[group][color].at[slots, pl.ds(source, size)],
                       got[group][color].at[slots, pl.ds(target, size)],
                       by_core(tp, functools.partial(flip, dp), color, stage))

    def reduce_send(group, color, stage, part):
        reduce_copy(group, color, stage, part).start()

    def reduce_add(group, color, stage, part):
        reduce_copy(group, color, stage, part).wait()
        slots, offset, into, size = cut(group, color, stage, part)
        kept = start_of(color, stage + 1) + offset
        target = DP - (DP >> stage) + into
        step = 4

        def one(i, carry):
            for slot in range(slots.start, slots.stop):
                to = pl.ds(kept + step * i, step)
                red[group][color][slot, to] = (
                    red[group][color][slot, to] + got[group][color][slot, pl.ds(target + step * i, step)])
            return carry

        lax.fori_loop(0, size // step, one, 0)

    def direct_share(color, mask):
        share = own[color]
        for stage in range(3, DIMS):
            weight = 32 >> stage
            if mask & weight:
                share = share + weight * (1 - 2 * bit(color, stage))
        return share

    def direct_reduce(group, color, mask):
        return message(group, color, 4 + mask, red[group][color].at[:, pl.ds(direct_share(color, mask), 1)],
                       got[group][color].at[:, pl.ds(55 + mask, 1)], direct_device(color, mask))

    def direct_gather(group, color, mask):
        spot = gat[group][color].at[:, pl.ds(own[color], 1)]
        return message(group, color, 11 + mask, spot, spot, direct_device(color, mask))

    def update(group, color):
        for slot, (tensor, block) in enumerate(BLOCKS[group][color]):
            row, col = 16 * (block // 2), 128 * (block % 2)
            spot = (2 * group + tensor, slice(row, row + 16), slice(col, col + 128))
            layer = 1 - group
            old = (layer, *spot[1:])
            old_m, old_v = (m_in[old], v_in[old]) if tensor else (m_out[old], v_out[old])
            grad = red[group][color][slot, own[color]]
            for mask in range(1, 8):
                grad = grad + got[group][color][slot, 55 + mask]
            moment = BETA1 * old_m + (1.0 - BETA1) * grad
            second = BETA2 * old_v + (1.0 - BETA2) * grad * grad
            m_new[spot] = moment
            v_new[spot] = second
            direction = (moment / CORR_MOM) / (jnp.sqrt(second / CORR_VAR) + EPSILON)
            gat[group][color][slot, own[color]] = direction.astype(BF16)

    def eight(color, near, far):
        return start_of(color, 3) + near * 8 * (1 - 2 * bit(color, 2)) + far * 16 * (1 - 2 * bit(color, 1))

    def gather_copy(group, color, stage, near, far):
        spot = gat[group][color].at[:, pl.ds(eight(color, near, far), 8)]
        return message(group, color, 19 + (near if stage == 1 else 2 + near + 2 * far if stage == 0 else 6), spot, spot,
                       by_core(tp, functools.partial(flip, dp), color, stage))

    def gather_start(group, color):
        for stage in (2, 1, 0):
            gather_copy(group, color, stage, 0, 0).start()

    def gather_near(group, color):
        gather_copy(group, color, 2, 0, 0).wait()
        for stage in (1, 0):
            gather_copy(group, color, stage, 1, 0).start()

    def gather_far(group, color):
        for near in range(2):
            gather_copy(group, color, 1, near, 0).wait()
            gather_copy(group, color, 0, near, 1).start()

    def gather_end(group, color):
        for far in range(2):
            for near in range(2):
                gather_copy(group, color, 0, near, far).wait()

    def write_out(group, color):
        return pltpu.make_async_copy(gat[group][color], n_out[group][color], out_sem.at[group, color])

    def colors(function, *args):
        for color in range(COLORS):
            function(*args[:1], color, *args[1:])

    def take(group, color, stage, part, then):
        reduce_add(group, color, stage, part)
        for number in range(then):
            reduce_send(group, color, stage + 1, number)

    def direct_start(group, color):
        for mask in range(1, 8):
            direct_reduce(group, color, mask).start()

    def direct_end(group, color):
        for mask in range(1, 8):
            direct_reduce(group, color, mask).wait()
        update(group, color)
        for mask in range(1, 8):
            direct_gather(group, color, mask).start()

    def direct_gathered(group, color):
        for mask in range(1, 8):
            direct_gather(group, color, mask).wait()
        gather_start(group, color)

    def last_stage(group, color):
        reduce_add(group, color, 2, 0)
        direct_start(group, color)

    def finish(group, color):
        gather_end(group, color)
        write_out(group, color).start()

    def forward(slot):
        return sum(dot(h_buf[:, TILE * q : TILE * (q + 1)], w_buf[slot, q]) for q in QUARTERS).astype(BF16)

    def backward(slot):
        return sum(dot(g_buf[:, TILE * q : TILE * (q + 1)], w_buf[slot, q], 1, 1) for q in QUARTERS)

    x_copy.wait()

    def z0_step(tile, carry):
        slot = take_chunk(0, tile)
        z = forward(slot)
        z0_buf[:, columns(tile)] = z
        a_buf[:, columns(tile)] = gelu(z.astype(F32)).astype(BF16)
        return carry

    lax.fori_loop(0, CHUNKS, z0_step, 0)

    def h_step(n, carry):
        total = None
        for half in range(2):
            slot = take_chunk(1, 2 * n + half)
            for q in QUARTERS:
                at = 2048 * half + TILE * q
                term = dot(a_buf[:, at : at + TILE], w_buf[slot, q])
                total = term if total is None else total + term
        pair_send_tile(0, n, total)
        return carry

    lax.fori_loop(0, 4, h_step, 0)
    wait_pq(p_in, 0)
    split(dot(h_buf[...], pq_buf[0]), hp0)
    load_pq(p_in, 1, 0)
    g_copy.wait()
    wait_pq(q_out, 1)
    split(dot(g_buf[...], pq_buf[1]), gq1)
    load_pq(q_out, 0, 1)
    pair_add(0, h_buf)

    def z1_step(tile, carry):
        slot = take_chunk(2, tile)
        z = forward(slot)
        z1_buf[:, columns(tile)] = z
        project(gelu(z.astype(F32)).astype(BF16), gq1, 0, 0, tile)
        return carry

    lax.fori_loop(0, CHUNKS, z1_step, 0)
    colors(reduce_send, 0, 0, 0)
    wait_pq(p_in, 0)
    split(dot(h_buf[...], pq_buf[0]), hp1)

    def da1_step(tile, carry):
        slot = take_chunk(3, tile)
        d_act = backward(slot)
        dz = (gelu_grad(z1_buf[:, columns(tile)].astype(F32)) * d_act).astype(BF16)
        z1_buf[:, columns(tile)] = dz
        project(dz, hp1, 0, 1, tile)
        return carry

    lax.fori_loop(0, CHUNKS, da1_step, 0)
    colors(reduce_send, 0, 0, 1)

    def b_step(n, carry):
        total = None
        for half in range(2):
            slot = take_chunk(4, 2 * n + half)
            for q in QUARTERS:
                at = 2048 * half + TILE * q
                term = dot(z1_buf[:, at : at + TILE], w_buf[slot, q], 1, 1)
                total = term if total is None else total + term
        pair_send_tile(1, n, total)
        return carry

    lax.fori_loop(0, 4, b_step, 0)
    wait_pq(q_out, 1)
    pair_add(1, g_buf)
    split(dot(g_buf[...], pq_buf[1]), gq0)

    def da0_step(tile, carry):
        slot = take_chunk(5, tile)

        @pl.when(tile == 1)
        def _():
            colors(take, 0, 0, 0, 0)
            colors(take, 0, 0, 1, 2)

        project(a_buf[:, columns(tile)], gq0, 1, 0, tile)
        d_act = backward(slot)
        dz = (gelu_grad(z0_buf[:, columns(tile)].astype(F32)) * d_act).astype(BF16)
        project(dz, hp0, 1, 1, tile)
        return carry

    lax.fori_loop(0, CHUNKS, da0_step, 0)

    colors(reduce_send, 1, 0, 0)
    colors(take, 0, 1, 0, 1)
    colors(reduce_send, 1, 0, 1)
    colors(take, 0, 1, 1, 0)
    colors(take, 1, 0, 0, 2)
    colors(last_stage, 0)
    colors(take, 1, 0, 1, 0)
    colors(take, 1, 1, 0, 1)
    colors(direct_end, 0)
    colors(take, 1, 1, 1, 0)
    colors(direct_gathered, 0)
    colors(last_stage, 1)
    colors(gather_near, 0)
    colors(direct_end, 1)
    colors(gather_far, 0)
    colors(direct_gathered, 1)
    colors(finish, 0)
    colors(gather_near, 1)
    colors(gather_far, 1)
    colors(finish, 1)
    for group in range(2):
        for color in range(COLORS):
            write_out(group, color).wait()


READS = 3
WRITES = 2


def apply_kernel(w_in, w_out, p_in, q_out, m_step, v_step, *rest):
    rest = iter(rest)
    shares = [next(rest) for item in range(6)]
    in_new, out_new, m_in, v_in, m_out, v_out = (next(rest) for item in range(6))
    gat = [next(rest) for item in range(6)]
    (p_buf, q_buf, in_read, out_read, in_write, out_write, n_buf,
     share_sem, basis_sem, read_sem, write_sem) = rest
    tp = lax.axis_index("tp")
    pairs = 2 * CHUNKS

    def tile_of(ref, pair, rows):
        layer = 1 - lax.div(pair, CHUNKS)
        at = pl.ds(pl.multiple_of(TILE * lax.rem(pair, CHUNKS), TILE), TILE)
        return ref.at[layer, at] if rows else ref.at[layer, :, at]

    def read(pair, rows):
        ref, buf = (w_out, out_read) if rows else (w_in, in_read)
        slot = lax.rem(pair, READS)
        return pltpu.make_async_copy(tile_of(ref, pair, rows), buf.at[slot], read_sem.at[rows, slot])

    def write(pair, rows):
        ref, buf = (out_new, out_write) if rows else (in_new, in_write)
        slot = lax.rem(pair, WRITES)
        return pltpu.make_async_copy(buf.at[slot], tile_of(ref, pair, rows), write_sem.at[rows, slot])

    def share_copy(item):
        return pltpu.make_async_copy(shares[item], gat[item], share_sem.at[item])

    def basis_copy(layer, rows):
        ref, buf = (q_out, q_buf) if rows else (p_in, p_buf)
        return pltpu.make_async_copy(ref.at[layer], buf.at[layer], basis_sem.at[layer, rows])

    for group in range(2):
        for color in range(COLORS):
            share_copy(COLORS * group + color).start()
        for rows in (1, 0):
            basis_copy(1 - group, rows).start()
        for pair in range(1 if group == 0 else READS):
            if group == 0 or pair:
                for rows in (1, 0):
                    read(jnp.int32(pair), rows).start()

    for step, in_ref, out_ref in ((m_step, m_in, m_out), (v_step, v_in, v_out)):
        for layer in range(2):
            out_ref[layer] = step[2 - 2 * layer]
            in_ref[layer] = step[3 - 2 * layer]

    def gather(group, tile):
        for lane in range(8):
            lane_bits = step_bits(tile, lane)
            spots = [place(lane_bits, color, tp) for color in range(COLORS)]
            for tensor in range(2):
                for block in range(8):
                    color, slot = WHERE[group][tensor, block]
                    row, col = 64 * lane + 16 * (block // 2), 128 * (block % 2)
                    n_buf[tensor, row : row + 16, col : col + 128] = gat[COLORS * group + color][slot, spots[color]]

    def one(pair, carry):
        layer = 1 - lax.div(pair, CHUNKS)
        for group in range(2):

            @pl.when(pair == CHUNKS * group)
            def _():
                for color in range(COLORS):
                    share_copy(COLORS * group + color).wait()
                for rows in (1, 0):
                    basis_copy(1 - group, rows).wait()

            @pl.when(layer == 1 - group)
            def _():
                gather(group, lax.rem(pair, CHUNKS))

        for rows in (1, 0):
            source, target = (out_read, out_write) if rows else (in_read, in_write)
            read(pair, rows).wait()

            @pl.when(pair >= WRITES)
            def _():
                write(pair - WRITES, rows).wait()

            slot, to = lax.rem(pair, READS), lax.rem(pair, WRITES)
            for cut in QUARTERS:
                at = slice(TILE * cut, TILE * (cut + 1))
                if rows:
                    spot = (slice(None), at)
                    change = dot(n_buf[0], q_buf[layer, at, :], 1, 1)
                else:
                    spot = (at, slice(None))
                    change = dot(p_buf[layer, at, :], n_buf[1], 1, 1)
                target[(to, *spot)] = (source[(slot, *spot)].astype(F32) - STEP_SIZE * change).astype(BF16)
            write(pair, rows).start()

            @pl.when(pair + READS < pairs)
            def _():
                read(pair + READS, rows).start()

        return carry

    lax.fori_loop(0, pairs, one, 0)
    for back in range(WRITES):
        for rows in (1, 0):
            write(jnp.int32(pairs - WRITES + back), rows).wait()


def local_step(x_rows, g_rows, w_in, w_out, p_in, q_out, m_in, v_in, m_out, v_out):
    m_in, v_in = (jnp.swapaxes(moment, 1, 2) for moment in (m_in, v_in))
    any_spec = pl.BlockSpec(memory_space=pl.ANY)
    vmem_spec = pl.BlockSpec(memory_space=pltpu.VMEM)
    shares = [jax.ShapeDtypeStruct((len(items), DP, 16, 128), BF16) for colors in BLOCKS for items in colors]
    moments = jax.ShapeDtypeStruct((4, 64, RANK), F32)
    rows_buf, wide_buf = pltpu.VMEM((TOK, D), BF16), pltpu.VMEM((TOK, F), BF16)
    parts_buf = pltpu.VMEM((TOK, 3 * RANK), BF16)
    basis_buf = pltpu.VMEM((2, D, RANK), BF16)
    dma = pltpu.SemaphoreType.DMA
    results = pl.pallas_call(
        step_kernel,
        out_shape=shares + [moments, moments],
        in_specs=[any_spec] * 6 + [vmem_spec] * 4,
        out_specs=[any_spec] * 6 + [vmem_spec] * 2,
        scratch_shapes=[pltpu.VMEM(s.shape, F32) for s in shares]
        + [pltpu.VMEM((s.shape[0], DP - 1, 16, 128), F32) for s in shares]
        + [pltpu.VMEM(s.shape, BF16) for s in shares]
        + [rows_buf] * 2
        + [wide_buf] * 3
        + [pltpu.VMEM((SLOTS, 4, TILE, TILE), BF16), basis_buf]
        + [parts_buf] * 4
        + [dma((SLOTS,)), dma((2,)), dma((2,)), dma((2, 3)), dma((2, 4)), dma((2, 4)), dma((2, 3, 26)), dma((2, 3, 26))],
        compiler_params=pltpu.CompilerParams(
            collective_id=0, has_side_effects=True, vmem_limit_bytes=67_000_000),
        name="galore_step",
    )(x_rows, g_rows, w_in, w_out, p_in, q_out, m_in, v_in, m_out, v_out)
    in_tile, out_tile = (D, TILE), (TILE, D)
    w_in_new, w_out_new, m_in, v_in, m_out, v_out = pl.pallas_call(
        apply_kernel,
        out_shape=[jax.ShapeDtypeStruct(w.shape, w.dtype) for w in (w_in, w_out, m_in, v_in, m_out, v_out)],
        in_specs=[any_spec] * 4 + [vmem_spec] * 2 + [any_spec] * 6,
        out_specs=[any_spec] * 2 + [vmem_spec] * 4,
        scratch_shapes=[pltpu.VMEM(s.shape, BF16) for s in shares]
        + [basis_buf] * 2
        + [pltpu.VMEM((READS, *in_tile), BF16), pltpu.VMEM((READS, *out_tile), BF16)]
        + [pltpu.VMEM((WRITES, *in_tile), BF16), pltpu.VMEM((WRITES, *out_tile), BF16)]
        + [pltpu.VMEM((2, TILE, RANK), BF16), dma((6,)), dma((2, 2)), dma((2, READS)), dma((2, WRITES))],
        compiler_params=pltpu.CompilerParams(vmem_limit_bytes=60_000_000),
        name="galore_apply",
    )(w_in, w_out, p_in, q_out, *results[6:], *results[:6])
    m_in, v_in = (jnp.swapaxes(moment, 1, 2) for moment in (m_in, v_in))
    return w_in_new, w_out_new, m_in, v_in, m_out, v_out


def solution(mesh):
    weight_in_spec = P(None, None, "tp")
    weight_out_spec = P(None, "tp", None)
    moment_in_spec = P(None, None, ("tp", "dp"))
    moment_out_spec = P(None, ("tp", "dp"), None)
    return jax.shard_map(
        local_step,
        mesh=mesh,
        in_specs=(P("dp", None), P("dp", None), weight_in_spec, weight_out_spec, P(), P(),
                  moment_in_spec, moment_in_spec, moment_out_spec, moment_out_spec),
        out_specs=(weight_in_spec, weight_out_spec, moment_in_spec, moment_in_spec, moment_out_spec, moment_out_spec),
        check_vma=False,
    )
```

time: 250 us -> 219 us (0.88)
  Pallas kernels: 239 us -> 217 us
  local copies, waits for them, and re-layouts: 4.63 us -> 0 us
  other arithmetic: 4.1 us -> 0 us
    pallas_call x1, Pallas kernels: 183 us -> 167 us  [local_step(): pl.pallas_call(step_kernel, out_shape=shares + [moments, moments], in_spe...]
    pallas_call x1, Pallas kernels: 56 us -> 50.3 us  [local_step(): pl.pallas_call(apply_kernel, out_shape=[jax.ShapeDtypeStruct(w.shape, w.d...]
    another operation x6 -> x0, other arithmetic: 4.1 us -> none  [the longest x2 1.45 us: gathered(): return jnp.stack([outs[1], ins[1].T, outs[0], ins[0].T])]
    slice x3 -> x0, local copies, waits for them, and re-layouts: 2.87 us -> none  [the longest x2 1.76 us: gathered(): return jnp.stack([outs[1], ins[1].T, outs[0], ins[0].T])]
where the time goes in v2:
time: 219 us; the launch traced here: 218 us
  Pallas kernels  217 us (99%)
    pallas_call x1, Pallas kernels, local_step(): pl.pallas_call(step_kernel, out_shape=shares + [moments, moments], in_spe...  167 us
    pallas_call x1, Pallas kernels, local_step(): pl.pallas_call(apply_kernel, out_shape=[jax.ShapeDtypeStruct(w.shape, w.d...  50.3 us

profile of v2, /device:TPU:0, one launch (start us, length us, event | category | flops | bytes accessed | tf_op | source)
XLA Modules:
  0.0 217.6 jit_solution(13243560320342109443)
XLA Ops:
  0.6 166.6 %galore_step.1 = (bf16[5,64,16,128]{3,2,1,0:T(8,128)(2,1)}, bf16[5,64,16,128]{3,2,1,0:T(8,128)(2,1)}, bf16[6,64,16,128]{3,2,1,0:T(8,128)(2,1)}, bf16[6,64,16,128...) custom-call(bf16[256,2048]{1,0:T(8,128)(2,1)} %x_hbm.1, ...), custom_call_target="tpu_custom_call" | custom-call | tf_op jit(solution)/shard_map/galore_step/pallas_call | solution.py:629
  167.3 50.3 %galore_apply.1 = (bf16[2,2048,4096]{2,1,0:T(8,128)(2,1)}, bf16[2,4096,2048]{2,1,0:T(8,128)(2,1)}, f32[2,64,256]{2,1,0:T(8,128)}, f32[2,64,256]{2,1,0:T(8,128)},...) custom-call(bf16[2,2048,4096]{2,1,0:T(8,128)(2,1)} %w_in.3, bf16[2,4096,2048]{2,1,0:T(8,128)(2,1)} %w_out.3, ...), custom_call_target="tpu_custom_call" | custom-call | tf_op jit(solution)/shard_map/galore_apply/pallas_call | solution.py:647

commit v3 on v2

--- a/solution.py
+++ b/solution.py
@@ -127,19 +127,6 @@
             ends.append(end)
         return ends[0] * (1 - tp) + ends[1] * tp
 
-    barrier = pltpu.get_barrier_semaphore()
-    greeted = set()
-    for color in range(COLORS):
-        for mask in range(1, 8):
-            dims = tuple(
-                tuple(sorted(stage_dim(color, stage, core) for stage in range(3, DIMS) if mask & (32 >> stage)))
-                for core in range(2))
-            if dims not in greeted:
-                greeted.add(dims)
-                pl.semaphore_signal(barrier, device_id={"dp": direct_device(color, mask)}, device_id_type=MESH)
-    pl.semaphore_signal(barrier, device_id={"tp": 1 - tp}, device_id_type=MESH)
-    pl.semaphore_wait(barrier, len(greeted) + 1)
-
     def block_of(phase, chunk, q):
         name, layer = phase
         half, rest_ = lax.rem(chunk, 2), lax.div(chunk, 2)
@@ -195,6 +182,18 @@
     load_pq(p_in, 0, 0)
     load_pq(q_out, 1, 1)
 
+    barrier = pltpu.get_barrier_semaphore()
+    greeted = set()
+    for color in range(COLORS):
+        for mask in range(1, 8):
+            dims = tuple(
+                tuple(sorted(stage_dim(color, stage, core) for stage in range(3, DIMS) if mask & (32 >> stage)))
+                for core in range(2))
+            if dims not in greeted:
+                greeted.add(dims)
+                pl.semaphore_signal(barrier, device_id={"dp": direct_device(color, mask)}, device_id_type=MESH)
+    pl.semaphore_signal(barrier, device_id={"tp": 1 - tp}, device_id_type=MESH)
+
     def split(values, out_ref):
         for part in range(3):
             piece = values.astype(BF16)
@@ -260,9 +259,10 @@
         every = slice(0, len(BLOCKS[group][color]))
         if stage == 2:
             return every, 0, 0, half
-        if group == 0 and stage == 0:
+        if stage == 0:
             first = FIRST_PART[color]
-            return (slice(first, every.stop) if part else slice(0, first)), 0, 0, half
+            every = slice(first, every.stop) if part >= 2 else slice(0, first)
+            part = part % 2
         ahead = bit(color, stage + 1)
         quarter = half // 2
         return every, (ahead if part else 1 - ahead) * quarter, part * quarter, quarter
@@ -271,7 +271,7 @@
         slots, offset, into, size = cut(group, color, stage, part)
         source = start_of(color, stage) + (1 - bit(color, stage)) * (32 >> stage) + offset
         target = DP - (DP >> stage) + into
-        return message(group, color, 2 * stage + part, red[group][color].at[slots, pl.ds(source, size)],
+        return message(group, color, part + 2 * stage + (2 if stage else 0), red[group][color].at[slots, pl.ds(source, size)],
                        got[group][color].at[slots, pl.ds(target, size)],
                        by_core(tp, functools.partial(flip, dp), color, stage))
 
@@ -303,12 +303,12 @@
         return share
 
     def direct_reduce(group, color, mask):
-        return message(group, color, 4 + mask, red[group][color].at[:, pl.ds(direct_share(color, mask), 1)],
+        return message(group, color, 6 + mask, red[group][color].at[:, pl.ds(direct_share(color, mask), 1)],
                        got[group][color].at[:, pl.ds(55 + mask, 1)], direct_device(color, mask))
 
     def direct_gather(group, color, mask):
         spot = gat[group][color].at[:, pl.ds(own[color], 1)]
-        return message(group, color, 11 + mask, spot, spot, direct_device(color, mask))
+        return message(group, color, 13 + mask, spot, spot, direct_device(color, mask))
 
     def update(group, color):
         for slot, (tensor, block) in enumerate(BLOCKS[group][color]):
@@ -332,7 +332,7 @@
 
     def gather_copy(group, color, stage, near, far):
         spot = gat[group][color].at[:, pl.ds(eight(color, near, far), 8)]
-        return message(group, color, 19 + (near if stage == 1 else 2 + near + 2 * far if stage == 0 else 6), spot, spot,
+        return message(group, color, 21 + (near if stage == 1 else 2 + near + 2 * far if stage == 0 else 6), spot, spot,
                        by_core(tp, functools.partial(flip, dp), color, stage))
 
     def gather_start(group, color):
@@ -365,6 +365,14 @@
         reduce_add(group, color, stage, part)
         for number in range(then):
             reduce_send(group, color, stage + 1, number)
+
+    def first_send(group, tensor):
+        for part in range(2):
+            colors(reduce_send, group, 0, 2 * tensor + part)
+
+    def first_take(group, color, kept):
+        take(group, color, 0, kept, 0)
+        take(group, color, 0, 2 + kept, 0 if kept else 2)
 
     def direct_start(group, color):
         for mask in range(1, 8):
@@ -406,6 +414,7 @@
         return carry
 
     lax.fori_loop(0, CHUNKS, z0_step, 0)
+    pl.semaphore_wait(barrier, len(greeted) + 1)
 
     def h_step(n, carry):
         total = None
@@ -436,7 +445,7 @@
         return carry
 
     lax.fori_loop(0, CHUNKS, z1_step, 0)
-    colors(reduce_send, 0, 0, 0)
+    first_send(0, 0)
     wait_pq(p_in, 0)
     split(dot(h_buf[...], pq_buf[0]), hp1)
 
@@ -449,7 +458,7 @@
         return carry
 
     lax.fori_loop(0, CHUNKS, da1_step, 0)
-    colors(reduce_send, 0, 0, 1)
+    first_send(0, 1)
 
     def b_step(n, carry):
         total = None
@@ -467,15 +476,17 @@
     pair_add(1, g_buf)
     split(dot(g_buf[...], pq_buf[1]), gq0)
 
+    def out_step(tile, carry):
+        project(a_buf[:, columns(tile)], gq0, 1, 0, tile)
+        return carry
+
+    lax.fori_loop(0, CHUNKS, out_step, 0)
+    first_send(1, 0)
+    colors(first_take, 0, 0)
+    colors(first_take, 0, 1)
+
     def da0_step(tile, carry):
         slot = take_chunk(5, tile)
-
-        @pl.when(tile == 1)
-        def _():
-            colors(take, 0, 0, 0, 0)
-            colors(take, 0, 0, 1, 2)
-
-        project(a_buf[:, columns(tile)], gq0, 1, 0, tile)
         d_act = backward(slot)
         dz = (gelu_grad(z0_buf[:, columns(tile)].astype(F32)) * d_act).astype(BF16)
         project(dz, hp0, 1, 1, tile)
@@ -483,13 +494,13 @@
 
     lax.fori_loop(0, CHUNKS, da0_step, 0)
 
-    colors(reduce_send, 1, 0, 0)
+    colors(reduce_send, 1, 0, 2)
     colors(take, 0, 1, 0, 1)
-    colors(reduce_send, 1, 0, 1)
+    colors(reduce_send, 1, 0, 3)
     colors(take, 0, 1, 1, 0)
-    colors(take, 1, 0, 0, 2)
+    colors(first_take, 1, 0)
     colors(last_stage, 0)
-    colors(take, 1, 0, 1, 0)
+    colors(first_take, 1, 1)
     colors(take, 1, 1, 0, 1)
     colors(direct_end, 0)
     colors(take, 1, 1, 1, 0)
@@ -638,7 +649,7 @@
         + [wide_buf] * 3
         + [pltpu.VMEM((SLOTS, 4, TILE, TILE), BF16), basis_buf]
         + [parts_buf] * 4
-        + [dma((SLOTS,)), dma((2,)), dma((2,)), dma((2, 3)), dma((2, 4)), dma((2, 4)), dma((2, 3, 26)), dma((2, 3, 26))],
+        + [dma((SLOTS,)), dma((2,)), dma((2,)), dma((2, 3)), dma((2, 4)), dma((2, 4)), dma((2, 3, 28)), dma((2, 3, 28))],
         compiler_params=pltpu.CompilerParams(
             collective_id=0, has_side_effects=True, vmem_limit_bytes=67_000_000),
         name="galore_step",

time: 219 us -> 207 us (0.945)
  Pallas kernels: 217 us -> 205 us
    pallas_call x1, Pallas kernels: 167 us -> 155 us  [local_step(): pl.pallas_call(step_kernel, out_shape=shares + [moments, moments], in_spe...]
where the time goes in v3:
time: 207 us; the launch traced here: 205 us
  Pallas kernels  205 us (99%)
    pallas_call x1, Pallas kernels, local_step(): pl.pallas_call(step_kernel, out_shape=shares + [moments, moments], in_spe...  155 us
    pallas_call x1, Pallas kernels, local_step(): pl.pallas_call(apply_kernel, out_shape=[jax.ShapeDtypeStruct(w.shape, w.d...  50.3 us

profile of v3, /device:TPU:0, one launch (start us, length us, event | category | flops | bytes accessed | tf_op | source)
XLA Modules:
  0.0 205.4 jit_solution(12032611103688091196)
XLA Ops:
  0.6 154.6 %galore_step.1 = (bf16[5,64,16,128]{3,2,1,0:T(8,128)(2,1)}, bf16[5,64,16,128]{3,2,1,0:T(8,128)(2,1)}, bf16[6,64,16,128]{3,2,1,0:T(8,128)(2,1)}, bf16[6,64,16,128...) custom-call(bf16[256,2048]{1,0:T(8,128)(2,1)} %x_hbm.1, ...), custom_call_target="tpu_custom_call" | custom-call | tf_op jit(solution)/shard_map/galore_step/pallas_call | solution.py:640
  155.2 50.3 %galore_apply.1 = (bf16[2,2048,4096]{2,1,0:T(8,128)(2,1)}, bf16[2,4096,2048]{2,1,0:T(8,128)(2,1)}, f32[2,64,256]{2,1,0:T(8,128)}, f32[2,64,256]{2,1,0:T(8,128)},...) custom-call(bf16[2,2048,4096]{2,1,0:T(8,128)(2,1)} %w_in.3, bf16[2,4096,2048]{2,1,0:T(8,128)(2,1)} %w_out.3, ...), custom_call_target="tpu_custom_call" | custom-call | tf_op jit(solution)/shard_map/galore_apply/pallas_call | solution.py:658
